TPU v7x, 256 devices: a whole 4x4x8 slice. The times are simulated.
256 devices in a mesh: rep: 2 (over x_hi), shard: 128 (over z, x_lo, y, core).
Axes of the slice: x: 4 (x_hi: 2, x_lo: 2; x = x_hi * 2 + x_lo), y: 4, z: 8, core: 2. Of those that a mesh axis runs over, the one named last changes fastest.
Arguments:
- tokens_x: bfloat16 [65536, 4096], P(('rep', 'shard')), may hold values from -24 to 24
- key_grad: bfloat16 [65536, 1024], P(('rep', 'shard')), may hold values from -0.0234375 to 0.0234375
- left_root: bfloat16 [512, 512, 512], P('shard'), may hold values from -1 to 3
- slot_grads: bfloat16 [512, 512, 512], P('shard'), may hold values from -6 to 6
- right_root: bfloat16 [512, 512, 512], P('shard'), may hold values from -1 to 3
- block_slot: int32 [256], replicated, may hold values from 0 to 511, as said below
Outputs:
- grad_key: float32 [4096, 1024], P('shard')
- update: bfloat16 [512, 256, 512], P('shard')
Inputs may be any that keep to these rules, and one draw needn't show every extreme that they name: `block_slot`: the entries are distinct; slot v is slot v % 4 of shard index v // 4; no shard index holds more than 4 blocks, and some shard index holds exactly 4.
All inputs are finite; a program needn't handle non-finite values.
Results may differ from a plain program's by a relative error of at most 0.006.
Values may be sent and summed in bfloat16 or wider, within the bound.
A program may use at most 128 MiB of HBM per device.

v0:
```python
import jax
import jax.numpy as jnp
from jax import lax
from jax.sharding import Mesh
from jax.sharding import PartitionSpec as P

SHARD = ("shard_0", "shard_1", "shard_2", "shard_3")
REP_SHARD = ("rep", "shard_0", "shard_1", "shard_2", "shard_3")


def split_up(value, dim, size):
    shape = value.shape
    blocks = value.reshape(*shape[:dim], size, shape[dim] // size, *shape[dim + 1 :])
    return jnp.moveaxis(blocks, dim, 0)


def sent_and_summed(value, axis, dim):
    blocks = split_up(value, dim, lax.axis_size(axis))
    arrived = lax.all_to_all(blocks, axis, split_axis=0, concat_axis=0, tiled=True)
    return arrived.astype(jnp.float32).sum(axis=0)


def summed_rows(value, axes, dim):
    far, near = axes
    own = sent_and_summed(split_up(value, dim, lax.axis_size(far)), near, dim + 1)
    return jnp.sum(
        lax.all_to_all(own.astype(jnp.bfloat16), far, 0, 0, tiled=True).astype(jnp.float32), axis=0
    )


def from_everyone(value, axis):
    size = lax.axis_size(axis)
    return lax.all_to_all(
        jnp.broadcast_to(value[None], (size, *value.shape)), axis, 0, 0, tiled=True
    )


def over_copies(value, axis):
    return from_everyone(value, axis).sum(axis=0)


def column_term(features, cotangent):
    return lax.dot_general(
        features, cotangent, (((0,), (0,)), ((), ())), preferred_element_type=jnp.float32
    )


def precondition(left_block, grad_block, right_block):
    left_part = jnp.einsum(
        "sij,sjk->sik", left_block, grad_block, preferred_element_type=jnp.float32
    ).astype(jnp.bfloat16)
    return jnp.einsum(
        "sij,sjk->isk", left_part, right_block, preferred_element_type=jnp.float32
    ).astype(jnp.bfloat16)


def shards(tokens_x, key_grad, left_root, slot_grads, right_root, block_slot):
    own_rows = summed_rows(
        column_term(tokens_x, key_grad).astype(jnp.bfloat16),
        (("shard_0", "shard_1", "shard_2"), "shard_3"),
        0,
    )
    grad_key = over_copies(own_rows, "rep")
    product = precondition(left_root, slot_grads, right_root)
    received = lax.all_to_all(product, SHARD, split_axis=0, concat_axis=1, tiled=True)
    update = jnp.take(received, block_slot, axis=1)
    return (grad_key, update)


def solution(mesh):
    finer = Mesh(
        mesh.devices.reshape(mesh.shape["rep"], 8, 2, 4, 2),
        ("rep", "shard_0", "shard_1", "shard_2", "shard_3"),
    )
    in_specs = (
        P(REP_SHARD, None),
        P(REP_SHARD, None),
        P(SHARD, None, None),
        P(SHARD, None, None),
        P(SHARD, None, None),
        P(),
    )
    out_specs = (P(SHARD, None), P(SHARD, None, None))
    return jax.shard_map(
        shards, mesh=finer, in_specs=in_specs, out_specs=out_specs, check_vma=False
    )
```

profile of v0, /device:TPU:1, one launch (start us, length us, event | category | flops | bytes accessed | tf_op | source)
XLA Modules:
  0.0 213.9 jit_solution(1199654257480087073)
XLA Ops:
  0.6 0.0 copy-start
  0.6 1.6 copy-done
  2.2 6.6 %convolution_convert_fusion = bf16[4096,1024]{1,0:T(8,128)(2,1)} fusion(bf16[256,4096]{1,0:T(8,128)(2,1)S(1)} %copy-done, bf16[256,1024]{1,0:T(8,128)(2,1)} %param.7), kind=kOutput, calls=%fused_computation.3 | convolution fusion | flops 2151677952 | bytes 11010048 | tf_op jit(solution)/shard_map/dot_general | solution.py:43
  8.9 8.5 %copy.19 = bf16[64,2,32,1024]{3,2,0,1:T(8,128)(2,1)} copy(bf16[64,2,32,1024]{3,2,1,0:T(8,128)(2,1)} %bitcast.17) | data formatting | bytes 16777216 | tf_op jit(solution)/shard_map/reshape;reshape | solution.py:13
  17.3 10.1 %all-to-all-start = ((bf16[2,64,32,1024]{3,2,1,0:T(8,128)(2,1)}), bf16[2,64,32,1024]{3,2,1,0:T(8,128)(2,1)}, u32[]{:S(2)}, u32[]{:S(2)}) async-start(bf16[2,64,32,1024]{3,2,1,0:T(8,128)(2,1)} %bitcast.18), calls=%async_computation | async-start | bytes 16777216 | tf_op jit(solution)/shard_map/all_to_all | solution.py:19
  27.4 6.5 %convert_bitcast_fusion = bf16[512,4,512]{2,0,1:T(8,128)(2,1)} fusion(bf16[4,512,512]{2,1,0:T(8,128)(2,1)} %param.10, bf16[4,512,512]{2,1,0:T(8,128)(2,1)} %param.8, bf16[4,512,512]{2,1,0:T(8,128)(2,1)} %param.9), kind=kOutput, calls=%fused_computation.4 | convolution fusion | flops 2149580800 | bytes 8388608 | tf_op jit(solution)/shard_map/sij,sjk->isk/dot_general | solution.py:52
  33.9 4.5 %copy.15 = bf16[512,4,512]{2,1,0:T(4,128)(2,1)} copy(bf16[512,4,512]{2,0,1:T(8,128)(2,1)} %convert_bitcast_fusion) | data formatting | bytes 4194304 | tf_op jit(solution)/shard_map/convert_element_type | solution.py:54
  38.5 0.0 all-to-all-done
  38.5 12.2 %all-to-all-start.3 = ((bf16[512,4,512]{2,1,0:T(4,128)(2,1)}), bf16[512,4,512]{2,1,0:T(4,128)(2,1)}, u32[]{:S(2)}, u32[]{:S(2)}) async-start(bf16[512,4,512]{2,1,0:T(4,128)(2,1)} %copy.15), calls=%async_computation.3 | async-start | bytes 4194304 | tf_op jit(solution)/shard_map/all_to_all | solution.py:65
  50.8 9.1 %reduce_sum.30 = bf16[64,32,1024]{2,1,0:T(8,128)(2,1)} reduce(bf16[2,64,32,1024]{3,2,1,0:T(8,128)(2,1)} %all-to-all-done, bf16[]{:T(256)} %constant.14.clone.1), dimensions={0}, to_apply=%region_0.0 | reduce | flops 2097152 | bytes 12582914 | tf_op jit(solution)/shard_map/reduce_sum | solution.py:20
  59.8 0.0 copy-start.1
  59.8 41.7 %all-to-all-done.3 = bf16[512,4,512]{2,1,0:T(4,128)(2,1)} async-done(((bf16[512,4,512]{2,1,0:T(4,128)(2,1)}), bf16[512,4,512]{2,1,0:T(4,128)(2,1)}, u32[]{:S(2)}, u32[]{:S(2)}) %all-to-all-start.3) | async-done | bytes 2097184 | tf_op jit(solution)/shard_map/all_to_all | solution.py:65
  101.6 6.1 %all-to-all-start.1 = ((bf16[64,32,1024]{2,1,0:T(8,128)(2,1)}), bf16[64,32,1024]{2,1,0:T(8,128)(2,1)}, u32[]{:S(2)}, u32[]{:S(2)}) async-start(bf16[64,32,1024]{2,1,0:T(8,128)(2,1)} %reduce_sum.30), calls=%async_computation.1 | async-start | bytes 8388608 | tf_op jit(solution)/shard_map/all_to_all | solution.py:27
  107.7 0.0 copy-done.1
  107.7 4.1 %copy.16 = bf16[128,4,4,512]{3,1,2,0:T(4,128)(2,1)} copy(bf16[128,4,4,512]{3,2,1,0:T(4,128)(2,1)} %bitcast.3) | data formatting | bytes 4194304 | tf_op jit(solution)/shard_map/all_to_all | solution.py:65
  111.9 3.1 %gather_fusion = bf16[256,4,512]{2,1,0:T(4,128)(2,1)S(1)} fusion(bf16[4,512,512]{2,0,1:T(4,128)(2,1)} %bitcast.19, s32[1024]{0:T(1024)S(1)} %pad_clamp_fusion), kind=kCustom, calls=%fused_computation | custom fusion | bytes 2098176 | tf_op jit(solution)/shard_map/jit(_take)/gather | solution.py:66
  115.0 85.3 %all-to-all-done.1 = bf16[64,32,1024]{2,1,0:T(8,128)(2,1)} async-done(((bf16[64,32,1024]{2,1,0:T(8,128)(2,1)}), bf16[64,32,1024]{2,1,0:T(8,128)(2,1)}, u32[]{:S(2)}, u32[]{:S(2)}) %all-to-all-start.1) | async-done | bytes 4194336 | tf_op jit(solution)/shard_map/all_to_all | solution.py:27
  200.3 3.0 %convert_reduce_fusion = f32[32,1024]{1,0:T(8,128)S(1)} fusion(bf16[64,32,1024]{2,1,0:T(8,128)(2,1)} %all-to-all-done.1), kind=kLoop, calls=%fused_computation.2 | loop fusion | flops 4161536 | bytes 4325376 | tf_op jit(solution)/shard_map/reduce_sum | solution.py:26
  203.3 0.7 broadcast_in_dim.18
  204.0 3.7 %all-to-all-start.2 = ((f32[2,32,1024]{2,1,0:T(8,128)}), f32[2,32,1024]{2,1,0:T(8,128)S(1)}, u32[]{:S(2)}, u32[]{:S(2)}) async-start(f32[2,32,1024]{2,1,0:T(8,128)} %broadcast_in_dim.18), calls=%async_computation.2 | async-start | bytes 524288 | tf_op jit(solution)/shard_map/all_to_all | solution.py:33
  207.7 1.0 select_bitcast_fusion
  208.8 1.2 copy.17
  209.9 3.3 %all-to-all-done.2 = f32[2,32,1024]{2,1,0:T(8,128)S(1)} async-done(((f32[2,32,1024]{2,1,0:T(8,128)}), f32[2,32,1024]{2,1,0:T(8,128)S(1)}, u32[]{:S(2)}, u32[]{:S(2)}) %all-to-all-start.2) | async-done | bytes 262176 | tf_op jit(solution)/shard_map/all_to_all | solution.py:33
  213.3 0.7 reduce_sum.32
  (3 shorter events, 0.0 us)
Async XLA Ops:
  0.6 1.6 copy-start
  17.3 21.2 %all-to-all-start = ((bf16[2,64,32,1024]{3,2,1,0:T(8,128)(2,1)}), bf16[2,64,32,1024]{3,2,1,0:T(8,128)(2,1)}, u32[]{:S(2)}, u32[]{:S(2)}) async-start(bf16[2,64,32,1024]{3,2,1,0:T(8,128)(2,1)} %bitcast.18), calls=%async_computation | async-start | bytes 16777216 | tf_op jit(solution)/shard_map/all_to_all | solution.py:19
  38.5 63.1 %all-to-all-start.3 = ((bf16[512,4,512]{2,1,0:T(4,128)(2,1)}), bf16[512,4,512]{2,1,0:T(4,128)(2,1)}, u32[]{:S(2)}, u32[]{:S(2)}) async-start(bf16[512,4,512]{2,1,0:T(4,128)(2,1)} %copy.15), calls=%async_computation.3 | async-start | bytes 4194304 | tf_op jit(solution)/shard_map/all_to_all | solution.py:65
  59.8 47.8 %copy-start.1 = (s32[256]{0:T(256)S(1)}, s32[256]{0:T(256)}, u32[]{:S(2)}) copy-start(s32[256]{0:T(256)} %param.11) | copy-start | bytes 3076
  101.6 98.7 %all-to-all-start.1 = ((bf16[64,32,1024]{2,1,0:T(8,128)(2,1)}), bf16[64,32,1024]{2,1,0:T(8,128)(2,1)}, u32[]{:S(2)}, u32[]{:S(2)}) async-start(bf16[64,32,1024]{2,1,0:T(8,128)(2,1)} %reduce_sum.30), calls=%async_computation.1 | async-start | bytes 8388608 | tf_op jit(solution)/shard_map/all_to_all | solution.py:27
  204.0 9.2 %all-to-all-start.2 = ((f32[2,32,1024]{2,1,0:T(8,128)}), f32[2,32,1024]{2,1,0:T(8,128)S(1)}, u32[]{:S(2)}, u32[]{:S(2)}) async-start(f32[2,32,1024]{2,1,0:T(8,128)} %broadcast_in_dim.18), calls=%async_computation.2 | async-start | bytes 524288 | tf_op jit(solution)/shard_map/all_to_all | solution.py:33
where the time goes:
time: 218 us; the launch traced here: 214 us
  waiting for transfers between devices  130 us (60%)
  starting transfers between devices  32.1 us (15%)
  local copies, waits for them, and re-layouts  23.7 us (11%)
  other arithmetic  13.8 us (6%)
  matrix products  13.1 us (6%)
    all_to_all x1, waiting for transfers between devices, summed_rows(): lax.all_to_all(own.astype(jnp.bfloat16), far, 0, 0, tiled=True)  85.3 us
    all_to_all x1, waiting for transfers between devices, shards(): lax.all_to_all(product, SHARD, split_axis=0, concat_axis=1, tiled=True)  41.7 us
    all_to_all x1, starting transfers between devices, shards(): lax.all_to_all(product, SHARD, split_axis=0, concat_axis=1, tiled=True)  12.2 us
    all_to_all x1, starting transfers between devices, sent_and_summed(): lax.all_to_all(blocks, axis, split_axis=0, concat_axis=0, tiled=True)  10.1 us
    reduce_sum x1, other arithmetic, sent_and_summed(): return arrived.astype(jnp.float32).sum(axis=0)  9.09 us
    another operation x1, local copies, waits for them, and re-layouts, split_up(): value.reshape(*shape[:dim], size, shape[dim] // size, *shape[dim + 1:])  8.46 us
    dot_general x1, matrix products, column_term(): lax.dot_general(features, cotangent, (((0,), (0,)), ((), ())), preferred_...  6.64 us
    dot_general x1, matrix products, precondition(): jnp.einsum('sij,sjk->isk', left_part, right_block, preferred_element_type...  6.5 us
  transfers between devices with their start and end apart: 4, of which 3 were waited for; matrix products, arithmetic and copies ran while one was open for 14% of the time, Pallas kernels for 0%

commit v1 on v0

v1 whole, which is shorter than its diff:
```python
import functools

import jax
import jax.numpy as jnp
from jax import lax
from jax.experimental import pallas as pl
from jax.experimental.pallas import tpu as pltpu
from jax.sharding import Mesh
from jax.sharding import PartitionSpec as P

AXES = ("rep", "shard_0", "shard_1", "shard_2", "shard_3")
SHARD = AXES[1:]
MESH = pl.DeviceIdType.MESH
F32 = jnp.float32
BF16 = jnp.bfloat16
NZ, NX, NY = 8, 4, 4
NSH = 128


def dot(a, b):
    return lax.dot_general(a, b, (((1,), (0,)), ((), ())), preferred_element_type=F32)


def dot_t(a, b):
    return lax.dot_general(a, b, (((0,), (0,)), ((), ())), preferred_element_type=F32)


def iota(shape, dim):
    return lax.broadcasted_iota(jnp.int32, shape, dim)


def drain(ref, sem):
    pltpu.make_async_copy(ref, ref, sem).wait()


def kernel(
    x_hbm, kg_hbm, left_hbm, grads_hbm, right_hbm, slot_ref,
    gk_out, up_out,
    xs, kgs, left_v, grads_v, right_v,
    t1, r1, s1, r2, s2, r3, fin,
    prod, recv, own, comp, comp_in, upd,
    x_sem, x_rsem, kg_sem, w_sem,
    send_core, send_key, send1, send2, send3, sem1, sem2, sem3, send_f, sem_f, loc_f,
    send_a, sem_a, send_c, sem_c, out_sem,
):
    e = lax.axis_index("rep")
    z = lax.axis_index("shard_0")
    l = lax.axis_index("shard_1")
    y = lax.axis_index("shard_2")
    c = lax.axis_index("shard_3")
    xp = e * 2 + l
    me = ((z * 2 + l) * 4 + y) * 2 + c
    partner = (e, z, l, y, 1 - c)

    def remote(src, dst, send_sem, recv_sem, device):
        pltpu.make_async_remote_copy(
            src_ref=src, dst_ref=dst, send_sem=send_sem, recv_sem=recv_sem,
            device_id=device, device_id_type=MESH,
        ).start()

    weights = ((left_hbm, left_v), (grads_hbm, grads_v), (right_hbm, right_v))
    for i, (src, dst) in enumerate(weights):
        pltpu.make_async_copy(src, dst, w_sem.at[i]).start()
    my_rows = pl.ds(pl.multiple_of(c * 256, 256), 256)

    def key_half(which):
        return kg_hbm.at[:, pl.ds(pl.multiple_of(which * 512, 512), 512)]

    remote(key_half(1 - c), kgs.at[my_rows, :], send_key, kg_sem.at[1], partner)
    pltpu.make_async_copy(key_half(c), kgs.at[my_rows, :], kg_sem.at[0]).start()

    def z_of(k):
        return lax.rem(z + 1 + k, NZ)

    def x_piece(k):
        return x_hbm.at[:, pl.ds(pl.multiple_of(z_of(k) * 512, 512), 512)]

    def fetch(k, carry):
        remote(x_piece(k), xs.at[k, my_rows, :], send_core, x_rsem.at[k], partner)
        pltpu.make_async_copy(x_piece(k), xs.at[k, my_rows, :], x_sem.at[k]).start()
        return carry

    lax.fori_loop(0, NZ, fetch, 0)

    slot_row = slot_ref[...]
    eye = iota((256, 256), 0) == iota((256, 256), 1)
    row_b = jnp.broadcast_to(slot_row, (256, 256))
    slot_col = jnp.sum(jnp.where(eye, row_b, 0), axis=1, keepdims=True)
    col_b = jnp.broadcast_to(slot_col, (256, 256))
    same = (row_b >> 2) == (col_b >> 2)
    less_r = col_b < row_b
    less_c = row_b < col_b
    g_row = jnp.sum(jnp.where(less_r, 1, 0), axis=0, keepdims=True)
    k_row = jnp.sum(jnp.where(less_r & same, 1, 0), axis=0, keepdims=True)
    g_col = jnp.sum(jnp.where(less_c, 1, 0), axis=1, keepdims=True)
    k_col = jnp.sum(jnp.where(less_c & same, 1, 0), axis=1, keepdims=True)
    mine_row = (g_row & 1) == e
    mine_col = (g_col & 1) == e

    for i, (src, dst) in enumerate(weights):
        pltpu.make_async_copy(src, dst, w_sem.at[i]).wait()
    parts = []
    for j in range(2):
        hit = mine_row & ((slot_row >> 2) == me) & ((k_row >> 1) == j)
        s = jnp.sum(jnp.where(hit, slot_row & 3, 0))
        half = dot(left_v[s], grads_v[s]).astype(BF16)
        parts.append(dot(half, right_v[s]).astype(BF16))

    out_row = iota((256, 256), 0)
    source = ((out_row >> 2) & 1) * 128 + (out_row >> 3) * 4 + (out_row & 3)
    perm = jnp.where(source == iota((256, 256), 1), 1.0, 0.0).astype(BF16)
    for q in range(4):
        stacked = jnp.concatenate([p[q * 128 : (q + 1) * 128] for p in parts], axis=0)
        moved = dot(perm, stacked).astype(BF16)
        prod[pl.ds(q * 32, 32)] = moved.reshape(32, 8, 512)

    def send_rows(i, carry):
        tz = lax.rem(z + lax.rem(i, 8), 8)
        tl = lax.rem(l + lax.rem(i // 8, 2), 2)
        ty = lax.rem(y + lax.rem(i // 16, 4), 4)
        tc = lax.rem(c + i // 64, 2)
        there = ((tz * 2 + tl) * 4 + ty) * 2 + tc
        remote(prod.at[there], recv.at[me], send_a, sem_a, (e, tz, tl, ty, tc))
        return carry

    lax.fori_loop(1, NSH, send_rows, 0)
    recv[me] = prod[me]

    drain(kgs.at[my_rows, :], kg_sem.at[0])
    drain(kgs.at[my_rows, :], kg_sem.at[1])

    def x_dev(p):
        return (p // 2, z, lax.rem(p, 2), y, c)

    def y_dev(p):
        return (e, z, l, p, c)

    def multiply(k, carry):
        drain(xs.at[k, my_rows, :], x_sem.at[k])
        drain(xs.at[k, my_rows, :], x_rsem.at[k])
        acc = dot_t(xs[k], kgs[...])
        for xl in range(2):
            for yy in range(NY):
                for xe in range(2):
                    base = (xl * 4 + yy) * 64
                    cols = slice(xe * 256, (xe + 1) * 256)
                    t1[k, 0, yy, xe * 2 + xl] = acc[base : base + 32, cols].astype(BF16)
                    t1[k, 1, xe * 2 + xl, yy] = acc[base + 32 : base + 64, cols].astype(BF16)
        for o in range(1, 4):
            to_y, to_x = lax.rem(y + o, 4), lax.rem(xp + o, 4)
            remote(t1.at[k, 0, to_y], r1.at[k, 0, o - 1], send1, sem1.at[k], y_dev(to_y))
            remote(t1.at[k, 1, to_x], r1.at[k, 1, o - 1], send1, sem1.at[k], x_dev(to_x))
        return carry

    lax.fori_loop(0, NZ, multiply, 0)

    def first_sum(k):
        drain(r1.at[k], sem1.at[k])
        for h, at in enumerate((y, xp)):
            total = t1[k, h, at].astype(F32)
            for o in range(3):
                total = total + r1[k, h, o].astype(F32)
            s1[k, h] = total.astype(BF16)
        for o in range(1, 4):
            to_y, to_x = lax.rem(y + o, 4), lax.rem(xp + o, 4)
            remote(s1.at[k, 0, to_x], r2.at[k, 0, o - 1], send2, sem2.at[k], x_dev(to_x))
            remote(s1.at[k, 1, to_y], r2.at[k, 1, o - 1], send2, sem2.at[k], y_dev(to_y))

    def second_total(k, h, at):
        total = s1[k, h, at].astype(F32)
        for o in range(3):
            total = total + r2[k, h, o].astype(F32)
        return total

    def second_sum(k):
        drain(r2.at[k], sem2.at[k])
        for h, at in enumerate((xp, y)):
            s2[k, h] = second_total(k, h, at).astype(BF16)
        remote(s2.at[k], r3.at[k], send3, sem3, (e, z_of(k), l, y, c))

    def sums(k, carry):
        first_sum(k)

        @pl.when(k > 0)
        def _():
            second_sum(k - 1)

        return carry

    lax.fori_loop(0, NZ, sums, 0)

    drain(recv.at[pl.ds(0, NSH - 1)], sem_a)
    pick = jnp.where(
        ((g_row >> 1) == iota((128, 256), 0)) & mine_row, 1.0, 0.0
    ).astype(BF16)
    place = jnp.where(
        ((g_col >> 1) == iota((256, 128), 1)) & jnp.logical_not(mine_col), 1.0, 0.0
    ).astype(BF16)
    first = jnp.where(mine_col, ((slot_col >> 2) * 2 + (k_col >> 1)) * 4, -8)
    other_rep = (1 - e, z, l, y, c)

    def compact(r, carry):
        chosen = jnp.where(iota((256, 1024), 1) == first + r, 1.0, 0.0).astype(BF16)
        rows = dot(chosen, recv[...].reshape(1024, 512)).astype(BF16)
        own[r] = rows
        comp[r] = dot(pick, rows).astype(BF16)
        remote(comp.at[r], comp_in.at[r], send_c, sem_c.at[r], other_rep)
        return carry

    lax.fori_loop(0, 4, compact, 0)

    drain(r2.at[NZ - 1], sem2.at[NZ - 1])
    drain(r3, sem3)
    for h, at in enumerate((xp, y)):
        total = second_total(NZ - 1, h, at)
        for k in range(NZ - 1):
            total = total + r3[k, h].astype(F32)
        fin[h] = total
    here = gk_out.at[:, pl.ds(pl.multiple_of((c * 2 + e) * 256, 256), 256)]
    pltpu.make_async_copy(fin.at[c], here, loc_f).start()
    remote(fin.at[c], here, send_f, sem_f, (1 - e, z, l, y, c))
    remote(fin.at[1 - c], here, send_f, sem_f, (e, z, l, y, 1 - c))
    remote(fin.at[1 - c], here, send_f, sem_f, (1 - e, z, l, y, 1 - c))

    def assemble(r, carry):
        drain(comp_in.at[r], sem_c.at[r])
        upd[r] = (dot(place, comp_in[r]) + own[r].astype(F32)).astype(BF16)
        pltpu.make_async_copy(upd.at[r], up_out.at[r], out_sem).start()
        return carry

    lax.fori_loop(0, 4, assemble, 0)
    drain(upd, out_sem)
    drain(fin.at[0], loc_f)
    drain(gk_out.at[:, pl.ds(0, 768)], sem_f)
    drain(gk_out.at[:, pl.ds(0, 768)], send_f)
    drain(kgs.at[my_rows, :], send_key)
    drain(xs.at[:, my_rows, :], send_core)
    drain(r1, send1)
    drain(r2, send2)
    drain(r3, send3)
    drain(recv.at[pl.ds(0, NSH - 1)], send_a)
    drain(comp, send_c)


def shards(tokens_x, key_grad, left_root, slot_grads, right_root, block_slot):
    any_space = pl.BlockSpec(memory_space=pl.ANY)
    vmem = pltpu.VMEM
    dma = pltpu.SemaphoreType.DMA
    return pl.pallas_call(
        kernel,
        out_shape=(
            jax.ShapeDtypeStruct((32, 1024), F32),
            jax.ShapeDtypeStruct((4, 256, 512), BF16),
        ),
        in_specs=[any_space] * 5 + [pl.BlockSpec(memory_space=pltpu.VMEM)],
        out_specs=(any_space, any_space),
        scratch_shapes=[
            vmem((8, 512, 512), BF16),
            vmem((512, 512), BF16),
            vmem((4, 512, 512), BF16),
            vmem((4, 512, 512), BF16),
            vmem((4, 512, 512), BF16),
            vmem((8, 2, 4, 4, 32, 256), BF16),
            vmem((8, 2, 3, 4, 32, 256), BF16),
            vmem((8, 2, 4, 32, 256), BF16),
            vmem((8, 2, 3, 32, 256), BF16),
            vmem((7, 2, 32, 256), BF16),
            vmem((7, 2, 32, 256), BF16),
            vmem((2, 32, 256), F32),
            vmem((128, 8, 512), BF16),
            vmem((128, 8, 512), BF16),
            vmem((4, 256, 512), BF16),
            vmem((4, 128, 512), BF16),
            vmem((4, 128, 512), BF16),
            vmem((4, 256, 512), BF16),
            dma((8,)), dma((8,)), dma((2,)), dma((3,)),
            dma, dma, dma, dma, dma, dma((8,)), dma((8,)), dma, dma, dma, dma,
            dma, dma, dma, dma((4,)), dma,
        ],
        compiler_params=pltpu.CompilerParams(has_side_effects=True),
        cost_estimate=pl.CostEstimate(
            flops=6 * 10**9, bytes_accessed=10 * 2**20, transcendentals=0
        ),
    )(tokens_x, key_grad, left_root, slot_grads, right_root, block_slot.reshape(1, 256))


def solution(mesh):
    finer = Mesh(mesh.devices.reshape(mesh.shape["rep"], 8, 2, 4, 2), AXES)
    in_specs = (
        P(AXES, None),
        P(AXES, None),
        P(SHARD, None, None),
        P(SHARD, None, None),
        P(SHARD, None, None),
        P(),
    )
    out_specs = (P(SHARD, None), P(SHARD, None, None))
    return jax.shard_map(
        shards, mesh=finer, in_specs=in_specs, out_specs=out_specs, check_vma=False
    )
```

time: 218 us -> 93.7 us (0.43)
  the two profiles are of different devices: /device:TPU:1 before, /device:TPU:3 now
where the time goes in v1:
time: 93.7 us; the launch traced here: 93.6 us
  Pallas kernels  89.1 us (95%)
  local copies, waits for them, and re-layouts  3.83 us (4%)
    pallas_call x1, Pallas kernels, shards(): pl.pallas_call(kernel, out_shape=(jax.ShapeDtypeStruct((32, 1024), F32),...  89.1 us
    unnamed x2, local copies, waits for them, and re-layouts  3.83 us

profile of v1, /device:TPU:3, one launch (start us, length us, event | category | flops | bytes accessed | tf_op | source)
XLA Modules:
  0.0 93.6 jit_solution(9525642071434307942)
XLA Ops:
  0.6 89.1 %shard_map.77 = (f32[32,1024]{1,0:T(8,128)}, bf16[4,256,512]{2,1,0:T(8,128)(2,1)}) custom-call(bf16[256,4096]{1,0:T(8,128)(2,1)} %x_hbm.1, bf16[256,1024]{1,0:T(8,128)(2,1)} %kg_hbm.1, bf16[4,512,512]{2,1,0:T(8,128)(2,1)} %left_hbm.1, bf16[4,512,512]{2,1,0:T(8,128)(2,1)} %grads_hbm.1, bf16[4,512,512]{2,1,0:T(8,128)(2,1)} %right_hbm.1, s32[1,256]{1,0:T(1,128)} %bitcast.1), custom_call_target="tpu_custom_call" | custom-call | flops 6000000000 | bytes 10485760 | tf_op jit(solution)/shard_map/pallas_call | solution.py:249
  89.7 1.6 %copy.10 = f32[32,1024]{1,0:T(8,128)} copy(f32[32,1024]{1,0:T(8,128)} %get-tuple-element.4) | data formatting | bytes 262144
  91.3 2.3 %copy.11 = bf16[4,256,512]{2,1,0:T(8,128)(2,1)} copy(bf16[4,256,512]{2,1,0:T(8,128)(2,1)} %get-tuple-element.5) | data formatting | bytes 2097152

commit v2 on v1

--- a/solution.py
+++ b/solution.py
@@ -15,6 +15,8 @@
 BF16 = jnp.bfloat16
 NZ, NX, NY = 8, 4, 4
 NSH = 128
+LAGS = (2, 4, 6)
+COMPACT = 7
 
 
 def dot(a, b):
@@ -37,10 +39,10 @@
     x_hbm, kg_hbm, left_hbm, grads_hbm, right_hbm, slot_ref,
     gk_out, up_out,
     xs, kgs, left_v, grads_v, right_v,
-    t1, r1, s1, r2, s2, r3, fin,
+    t1, rel, cmb, r1, s1, r2, s2, r3, fin,
     prod, recv, own, comp, comp_in, upd,
     x_sem, x_rsem, kg_sem, w_sem,
-    send_core, send_key, send1, send2, send3, sem1, sem2, sem3, send_f, sem_f, loc_f,
+    send_core, send_key, send_rel, send_dir, send_cmb, send2, send3, sem_rel, sem1, sem2, sem3, send_f, sem_f, loc_f,
     send_a, sem_a, send_c, sem_c, out_sem,
 ):
     e = lax.axis_index("rep")
@@ -58,6 +60,30 @@
             device_id=device, device_id_type=MESH,
         ).start()
 
+    barrier = pltpu.get_barrier_semaphore()
+
+    def peer(k, m):
+        tz = lax.rem(z + k + m, NZ)
+        return (
+            e, tz, lax.rem(l + m % 2, 2), lax.rem(y + m // 2 % 4, 4), lax.rem(c + m // 8, 2)
+        )
+
+    def greet(there):
+        pl.semaphore_signal(barrier, inc=1, device_id=there, device_id_type=MESH)
+
+    def greet_all(k, carry):
+        @pl.when(k > 0)
+        def _():
+            greet(peer(k, 0))
+
+        for m in range(1, 16):
+            greet(peer(k, m))
+        return carry
+
+    for there in ((1 - e, z, l, y, c), (1 - e, z, l, y, 1 - c), (1 - e, z, 1 - l, y, c)):
+        greet(there)
+    lax.fori_loop(0, NZ, greet_all, 0)
+
     weights = ((left_hbm, left_v), (grads_hbm, grads_v), (right_hbm, right_v))
     for i, (src, dst) in enumerate(weights):
         pltpu.make_async_copy(src, dst, w_sem.at[i]).start()
@@ -66,7 +92,6 @@
     def key_half(which):
         return kg_hbm.at[:, pl.ds(pl.multiple_of(which * 512, 512), 512)]
 
-    remote(key_half(1 - c), kgs.at[my_rows, :], send_key, kg_sem.at[1], partner)
     pltpu.make_async_copy(key_half(c), kgs.at[my_rows, :], kg_sem.at[0]).start()
 
     def z_of(k):
@@ -76,11 +101,14 @@
         return x_hbm.at[:, pl.ds(pl.multiple_of(z_of(k) * 512, 512), 512)]
 
     def fetch(k, carry):
+        pltpu.make_async_copy(x_piece(k), xs.at[k, my_rows, :], x_sem.at[k]).start()
+        return carry
+
+    lax.fori_loop(0, NZ, fetch, 0)
+
+    def swap(k, carry):
         remote(x_piece(k), xs.at[k, my_rows, :], send_core, x_rsem.at[k], partner)
-        pltpu.make_async_copy(x_piece(k), xs.at[k, my_rows, :], x_sem.at[k]).start()
-        return carry
-
-    lax.fori_loop(0, NZ, fetch, 0)
+        return carry
 
     slot_row = slot_ref[...]
     eye = iota((256, 256), 0) == iota((256, 256), 1)
@@ -101,6 +129,10 @@
         pltpu.make_async_copy(src, dst, w_sem.at[i]).wait()
     parts = []
     for j in range(2):
+        if j == 1:
+            pl.semaphore_wait(barrier, NSH + 2)
+            remote(key_half(1 - c), kgs.at[my_rows, :], send_key, kg_sem.at[1], partner)
+            lax.fori_loop(0, NZ, swap, 0)
         hit = mine_row & ((slot_row >> 2) == me) & ((k_row >> 1) == j)
         s = jnp.sum(jnp.where(hit, slot_row & 3, 0))
         half = dot(left_v[s], grads_v[s]).astype(BF16)
@@ -114,82 +146,122 @@
         moved = dot(perm, stacked).astype(BF16)
         prod[pl.ds(q * 32, 32)] = moved.reshape(32, 8, 512)
 
-    def send_rows(i, carry):
-        tz = lax.rem(z + lax.rem(i, 8), 8)
-        tl = lax.rem(l + lax.rem(i // 8, 2), 2)
-        ty = lax.rem(y + lax.rem(i // 16, 4), 4)
-        tc = lax.rem(c + i // 64, 2)
+    def y_first(k, h):
+        return True if h == 0 else lax.rem(k, 4) == 0
+
+    def pick2(cond, a, b):
+        return a if cond is True else jnp.where(cond, a, b)
+
+    def ring(along_y, p):
+        return (
+            pick2(along_y, e, p // 2),
+            z,
+            pick2(along_y, l, lax.rem(p, 2)),
+            pick2(along_y, p, y),
+            c,
+        )
+
+    def other(along_y):
+        return False if along_y is True else jnp.logical_not(along_y)
+
+    def pos(along_y):
+        if along_y is False:
+            return xp
+        return pick2(along_y, y, xp)
+
+    def ring_of(along_y, p):
+        if along_y is False:
+            return (p // 2, z, lax.rem(p, 2), y, c)
+        return ring(along_y, p)
+
+    def step_to(p, o):
+        return lax.rem(p + o, 4)
+
+    lower, upper = pl.ds(0, 2), pl.ds(2, 2)
+
+    def send_rows(k, m):
+        device = peer(k, m)
+        _, tz, tl, ty, tc = device
         there = ((tz * 2 + tl) * 4 + ty) * 2 + tc
-        remote(prod.at[there], recv.at[me], send_a, sem_a, (e, tz, tl, ty, tc))
-        return carry
-
-    lax.fori_loop(1, NSH, send_rows, 0)
+        remote(prod.at[there], recv.at[me], send_a, sem_a, device)
+
+    def send_all(k, carry):
+        @pl.when(k > 0)
+        def _():
+            send_rows(k, 0)
+
+        for m in range(1, 16):
+            send_rows(k, m)
+        return carry
+
+    lax.fori_loop(0, NZ, send_all, 0)
     recv[me] = prod[me]
 
     drain(kgs.at[my_rows, :], kg_sem.at[0])
     drain(kgs.at[my_rows, :], kg_sem.at[1])
 
-    def x_dev(p):
-        return (p // 2, z, lax.rem(p, 2), y, c)
-
-    def y_dev(p):
-        return (e, z, l, p, c)
-
-    def multiply(k, carry):
+    def multiply(k):
         drain(xs.at[k, my_rows, :], x_sem.at[k])
         drain(xs.at[k, my_rows, :], x_rsem.at[k])
         acc = dot_t(xs[k], kgs[...])
-        for xl in range(2):
-            for yy in range(NY):
-                for xe in range(2):
-                    base = (xl * 4 + yy) * 64
-                    cols = slice(xe * 256, (xe + 1) * 256)
-                    t1[k, 0, yy, xe * 2 + xl] = acc[base : base + 32, cols].astype(BF16)
-                    t1[k, 1, xe * 2 + xl, yy] = acc[base + 32 : base + 64, cols].astype(BF16)
-        for o in range(1, 4):
-            to_y, to_x = lax.rem(y + o, 4), lax.rem(xp + o, 4)
-            remote(t1.at[k, 0, to_y], r1.at[k, 0, o - 1], send1, sem1.at[k], y_dev(to_y))
-            remote(t1.at[k, 1, to_x], r1.at[k, 1, o - 1], send1, sem1.at[k], x_dev(to_x))
-        return carry
-
-    lax.fori_loop(0, NZ, multiply, 0)
+        for h in range(2):
+            along_y = y_first(k, h)
+            for xl in range(2):
+                for yy in range(NY):
+                    for xe in range(2):
+                        base = (xl * 4 + yy) * 64 + h * 32
+                        cols = slice(xe * 256, (xe + 1) * 256)
+                        xx = xe * 2 + xl
+                        piece = acc[base : base + 32, cols].astype(BF16)
+                        t1[k, h, pick2(along_y, yy, xx), pick2(along_y, xx, yy)] = piece
+        for h in range(2):
+            along_y = y_first(k, h)
+            p = pos(along_y)
+            nxt, far, prv = step_to(p, 1), step_to(p, 2), step_to(p, 3)
+            to_n, to_p = ring_of(along_y, nxt), ring_of(along_y, prv)
+            remote(t1.at[k, h, far, lower], rel.at[k, h, 0], send_rel, sem_rel.at[k], to_n)
+            remote(t1.at[k, h, far, upper], rel.at[k, h, 1], send_rel, sem_rel.at[k], to_p)
+            remote(t1.at[k, h, nxt, upper], r1.at[k, h, 0, upper], send_dir, sem1.at[k], to_n)
+            remote(t1.at[k, h, prv, lower], r1.at[k, h, 1, lower], send_dir, sem1.at[k], to_p)
+
+    def relay(k):
+        drain(rel.at[k], sem_rel.at[k])
+        for h in range(2):
+            along_y = y_first(k, h)
+            p = pos(along_y)
+            nxt, prv = step_to(p, 1), step_to(p, 3)
+            half = t1[k, h, nxt, 0:2].astype(F32) + rel[k, h, 0].astype(F32)
+            cmb[k, h, 0] = half.astype(BF16)
+            remote(cmb.at[k, h, 0], r1.at[k, h, 0, lower], send_cmb, sem1.at[k], ring_of(along_y, nxt))
+            half = t1[k, h, prv, 2:4].astype(F32) + rel[k, h, 1].astype(F32)
+            cmb[k, h, 1] = half.astype(BF16)
+            remote(cmb.at[k, h, 1], r1.at[k, h, 1, upper], send_cmb, sem1.at[k], ring_of(along_y, prv))
 
     def first_sum(k):
         drain(r1.at[k], sem1.at[k])
-        for h, at in enumerate((y, xp)):
-            total = t1[k, h, at].astype(F32)
-            for o in range(3):
-                total = total + r1[k, h, o].astype(F32)
-            s1[k, h] = total.astype(BF16)
-        for o in range(1, 4):
-            to_y, to_x = lax.rem(y + o, 4), lax.rem(xp + o, 4)
-            remote(s1.at[k, 0, to_x], r2.at[k, 0, o - 1], send2, sem2.at[k], x_dev(to_x))
-            remote(s1.at[k, 1, to_y], r2.at[k, 1, o - 1], send2, sem2.at[k], y_dev(to_y))
-
-    def second_total(k, h, at):
-        total = s1[k, h, at].astype(F32)
+        for h in range(2):
+            along_y = y_first(k, h)
+            total = t1[k, h, pos(along_y)].astype(F32)
+            s1[k, h] = (total + r1[k, h, 0].astype(F32) + r1[k, h, 1].astype(F32)).astype(BF16)
+        for h in range(2):
+            along_y = other(y_first(k, h))
+            p = pos(along_y)
+            for o in (2, 1, 3):
+                to = step_to(p, o)
+                remote(s1.at[k, h, to], r2.at[k, h, o - 1], send2, sem2.at[k], ring_of(along_y, to))
+
+    def second_total(k, h):
+        total = s1[k, h, pos(other(y_first(k, h)))].astype(F32)
         for o in range(3):
             total = total + r2[k, h, o].astype(F32)
         return total
 
     def second_sum(k):
         drain(r2.at[k], sem2.at[k])
-        for h, at in enumerate((xp, y)):
-            s2[k, h] = second_total(k, h, at).astype(BF16)
+        for h in range(2):
+            s2[k, h] = second_total(k, h).astype(BF16)
         remote(s2.at[k], r3.at[k], send3, sem3, (e, z_of(k), l, y, c))
 
-    def sums(k, carry):
-        first_sum(k)
-
-        @pl.when(k > 0)
-        def _():
-            second_sum(k - 1)
-
-        return carry
-
-    lax.fori_loop(0, NZ, sums, 0)
-
-    drain(recv.at[pl.ds(0, NSH - 1)], sem_a)
     pick = jnp.where(
         ((g_row >> 1) == iota((128, 256), 0)) & mine_row, 1.0, 0.0
     ).astype(BF16)
@@ -199,20 +271,57 @@
     first = jnp.where(mine_col, ((slot_col >> 2) * 2 + (k_col >> 1)) * 4, -8)
     other_rep = (1 - e, z, l, y, c)
 
-    def compact(r, carry):
+    def compact(r):
         chosen = jnp.where(iota((256, 1024), 1) == first + r, 1.0, 0.0).astype(BF16)
         rows = dot(chosen, recv[...].reshape(1024, 512)).astype(BF16)
         own[r] = rows
         comp[r] = dot(pick, rows).astype(BF16)
         remote(comp.at[r], comp_in.at[r], send_c, sem_c.at[r], other_rep)
-        return carry
-
-    lax.fori_loop(0, 4, compact, 0)
+
+    def within(i, lag, count):
+        return (i >= lag) & (i < lag + count)
+
+    def steps(i, carry):
+        @pl.when(i < NZ)
+        def _():
+            multiply(i)
+
+        @pl.when(within(i, LAGS[0], NZ))
+        def _():
+            relay(i - LAGS[0])
+
+        @pl.when(within(i, LAGS[1], NZ))
+        def _():
+            first_sum(i - LAGS[1])
+
+        @pl.when(within(i, LAGS[2], NZ - 1))
+        def _():
+            second_sum(i - LAGS[2])
+
+        @pl.when(i == COMPACT)
+        def _():
+            drain(recv.at[pl.ds(0, NSH - 1)], sem_a)
+
+        @pl.when(within(i, COMPACT, 4))
+        def _():
+            compact(i - COMPACT)
+
+        return carry
+
+    lax.fori_loop(0, max(NZ + LAGS[1], NZ - 1 + LAGS[2]), steps, 0)
+
+    def assemble(r, carry):
+        drain(comp_in.at[r], sem_c.at[r])
+        upd[r] = (dot(place, comp_in[r]) + own[r].astype(F32)).astype(BF16)
+        pltpu.make_async_copy(upd.at[r], up_out.at[r], out_sem).start()
+        return carry
+
+    lax.fori_loop(0, 4, assemble, 0)
 
     drain(r2.at[NZ - 1], sem2.at[NZ - 1])
     drain(r3, sem3)
-    for h, at in enumerate((xp, y)):
-        total = second_total(NZ - 1, h, at)
+    for h in range(2):
+        total = second_total(NZ - 1, h)
         for k in range(NZ - 1):
             total = total + r3[k, h].astype(F32)
         fin[h] = total
@@ -222,20 +331,15 @@
     remote(fin.at[1 - c], here, send_f, sem_f, (e, z, l, y, 1 - c))
     remote(fin.at[1 - c], here, send_f, sem_f, (1 - e, z, l, y, 1 - c))
 
-    def assemble(r, carry):
-        drain(comp_in.at[r], sem_c.at[r])
-        upd[r] = (dot(place, comp_in[r]) + own[r].astype(F32)).astype(BF16)
-        pltpu.make_async_copy(upd.at[r], up_out.at[r], out_sem).start()
-        return carry
-
-    lax.fori_loop(0, 4, assemble, 0)
     drain(upd, out_sem)
     drain(fin.at[0], loc_f)
     drain(gk_out.at[:, pl.ds(0, 768)], sem_f)
     drain(gk_out.at[:, pl.ds(0, 768)], send_f)
     drain(kgs.at[my_rows, :], send_key)
     drain(xs.at[:, my_rows, :], send_core)
-    drain(r1, send1)
+    drain(rel, send_rel)
+    drain(rel, send_dir)
+    drain(cmb, send_cmb)
     drain(r2, send2)
     drain(r3, send3)
     drain(recv.at[pl.ds(0, NSH - 1)], send_a)
@@ -261,7 +365,9 @@
             vmem((4, 512, 512), BF16),
             vmem((4, 512, 512), BF16),
             vmem((8, 2, 4, 4, 32, 256), BF16),
-            vmem((8, 2, 3, 4, 32, 256), BF16),
+            vmem((8, 2, 2, 2, 32, 256), BF16),
+            vmem((8, 2, 2, 2, 32, 256), BF16),
+            vmem((8, 2, 2, 4, 32, 256), BF16),
             vmem((8, 2, 4, 32, 256), BF16),
             vmem((8, 2, 3, 32, 256), BF16),
             vmem((7, 2, 32, 256), BF16),
@@ -274,10 +380,10 @@
             vmem((4, 128, 512), BF16),
             vmem((4, 256, 512), BF16),
             dma((8,)), dma((8,)), dma((2,)), dma((3,)),
-            dma, dma, dma, dma, dma, dma((8,)), dma((8,)), dma, dma, dma, dma,
+            dma, dma, dma, dma, dma, dma, dma, dma((8,)), dma((8,)), dma((8,)), dma, dma, dma, dma,
             dma, dma, dma, dma((4,)), dma,
         ],
-        compiler_params=pltpu.CompilerParams(has_side_effects=True),
+        compiler_params=pltpu.CompilerParams(has_side_effects=True, collective_id=0),
         cost_estimate=pl.CostEstimate(
             flops=6 * 10**9, bytes_accessed=10 * 2**20, transcendentals=0
         ),

time: 93.7 us -> 73.7 us (0.79)
  the two profiles are of different devices: /device:TPU:3 before, /device:TPU:1 now
where the time goes in v2:
time: 73.7 us; the launch traced here: 73.6 us
  Pallas kernels  69.1 us (94%)
  local copies, waits for them, and re-layouts  3.83 us (5%)
    pallas_call x1, Pallas kernels, shards(): pl.pallas_call(kernel, out_shape=(jax.ShapeDtypeStruct((32, 1024), F32),...  69.1 us
    unnamed x2, local copies, waits for them, and re-layouts  3.83 us

profile of v2, /device:TPU:1, one launch (start us, length us, event | category | flops | bytes accessed | tf_op | source)
XLA Modules:
  0.0 73.6 jit_solution(17307835313725538722)
XLA Ops:
  0.6 69.1 %shard_map.77 = (f32[32,1024]{1,0:T(8,128)}, bf16[4,256,512]{2,1,0:T(8,128)(2,1)}) custom-call(bf16[256,4096]{1,0:T(8,128)(2,1)} %x_hbm.1, bf16[256,1024]{1,0:T(8,128)(2,1)} %kg_hbm.1, bf16[4,512,512]{2,1,0:T(8,128)(2,1)} %left_hbm.1, bf16[4,512,512]{2,1,0:T(8,128)(2,1)} %grads_hbm.1, bf16[4,512,512]{2,1,0:T(8,128)(2,1)} %right_hbm.1, s32[1,256]{1,0:T(1,128)} %bitcast.1), custom_call_target="tpu_custom_call" | custom-call | flops 6000000000 | bytes 10485760 | tf_op jit(solution)/shard_map/pallas_call | solution.py:353
  69.8 1.6 %copy.10 = f32[32,1024]{1,0:T(8,128)} copy(f32[32,1024]{1,0:T(8,128)} %get-tuple-element.4) | data formatting | bytes 262144
  71.3 2.3 %copy.11 = bf16[4,256,512]{2,1,0:T(8,128)(2,1)} copy(bf16[4,256,512]{2,1,0:T(8,128)(2,1)} %get-tuple-element.5) | data formatting | bytes 2097152

commit v3 on v2

--- a/solution.py
+++ b/solution.py
@@ -36,9 +36,9 @@
 
 
 def kernel(
-    x_hbm, kg_hbm, left_hbm, grads_hbm, right_hbm, slot_ref,
+    x_hbm, kg_hbm, left_hbm, grads_hbm, right_hbm, slot_hbm,
     gk_out, up_out,
-    xs, kgs, left_v, grads_v, right_v,
+    slot_ref, xs, kgs, left_v, grads_v, right_v,
     t1, rel, cmb, r1, s1, r2, s2, r3, fin,
     prod, recv, own, comp, comp_in, upd,
     x_sem, x_rsem, kg_sem, w_sem,
@@ -60,6 +60,12 @@
             device_id=device, device_id_type=MESH,
         ).start()
 
+    slots = pltpu.make_async_copy(slot_hbm, slot_ref, w_sem.at[3])
+    slots.start()
+    weights = ((left_hbm, left_v), (grads_hbm, grads_v), (right_hbm, right_v))
+    for i, (src, dst) in enumerate(weights):
+        pltpu.make_async_copy(src, dst, w_sem.at[i]).start()
+
     barrier = pltpu.get_barrier_semaphore()
 
     def peer(k, m):
@@ -84,9 +90,6 @@
         greet(there)
     lax.fori_loop(0, NZ, greet_all, 0)
 
-    weights = ((left_hbm, left_v), (grads_hbm, grads_v), (right_hbm, right_v))
-    for i, (src, dst) in enumerate(weights):
-        pltpu.make_async_copy(src, dst, w_sem.at[i]).start()
     my_rows = pl.ds(pl.multiple_of(c * 256, 256), 256)
 
     def key_half(which):
@@ -110,6 +113,7 @@
         remote(x_piece(k), xs.at[k, my_rows, :], send_core, x_rsem.at[k], partner)
         return carry
 
+    slots.wait()
     slot_row = slot_ref[...]
     eye = iota((256, 256), 0) == iota((256, 256), 1)
     row_b = jnp.broadcast_to(slot_row, (256, 256))
@@ -125,8 +129,8 @@
     mine_row = (g_row & 1) == e
     mine_col = (g_col & 1) == e
 
-    for i, (src, dst) in enumerate(weights):
-        pltpu.make_async_copy(src, dst, w_sem.at[i]).wait()
+    for i in range(2):
+        drain(left_v, w_sem.at[i])
     parts = []
     for j in range(2):
         if j == 1:
@@ -136,6 +140,8 @@
         hit = mine_row & ((slot_row >> 2) == me) & ((k_row >> 1) == j)
         s = jnp.sum(jnp.where(hit, slot_row & 3, 0))
         half = dot(left_v[s], grads_v[s]).astype(BF16)
+        if j == 0:
+            drain(right_v, w_sem.at[2])
         parts.append(dot(half, right_v[s]).astype(BF16))
 
     out_row = iota((256, 256), 0)
@@ -147,7 +153,7 @@
         prod[pl.ds(q * 32, 32)] = moved.reshape(32, 8, 512)
 
     def y_first(k, h):
-        return True if h == 0 else lax.rem(k, 4) == 0
+        return (k >= 0) if h == 0 else (k < 0)
 
     def pick2(cond, a, b):
         return a if cond is True else jnp.where(cond, a, b)
@@ -312,11 +318,10 @@
 
     def assemble(r, carry):
         drain(comp_in.at[r], sem_c.at[r])
-        upd[r] = (dot(place, comp_in[r]) + own[r].astype(F32)).astype(BF16)
-        pltpu.make_async_copy(upd.at[r], up_out.at[r], out_sem).start()
-        return carry
-
-    lax.fori_loop(0, 4, assemble, 0)
+        up_out[r] = (dot(place, comp_in[r]) + own[r].astype(F32)).astype(BF16)
+        return carry
+
+    lax.fori_loop(0, 3, assemble, 0)
 
     drain(r2.at[NZ - 1], sem2.at[NZ - 1])
     drain(r3, sem3)
@@ -331,7 +336,7 @@
     remote(fin.at[1 - c], here, send_f, sem_f, (e, z, l, y, 1 - c))
     remote(fin.at[1 - c], here, send_f, sem_f, (1 - e, z, l, y, 1 - c))
 
-    drain(upd, out_sem)
+    assemble(3, 0)
     drain(fin.at[0], loc_f)
     drain(gk_out.at[:, pl.ds(0, 768)], sem_f)
     drain(gk_out.at[:, pl.ds(0, 768)], send_f)
@@ -356,9 +361,10 @@
             jax.ShapeDtypeStruct((32, 1024), F32),
             jax.ShapeDtypeStruct((4, 256, 512), BF16),
         ),
-        in_specs=[any_space] * 5 + [pl.BlockSpec(memory_space=pltpu.VMEM)],
-        out_specs=(any_space, any_space),
+        in_specs=[any_space] * 6,
+        out_specs=(pl.BlockSpec(memory_space=pltpu.VMEM), pl.BlockSpec(memory_space=pltpu.VMEM)),
         scratch_shapes=[
+            vmem((1, 256), jnp.int32),
             vmem((8, 512, 512), BF16),
             vmem((512, 512), BF16),
             vmem((4, 512, 512), BF16),
@@ -379,11 +385,11 @@
             vmem((4, 128, 512), BF16),
             vmem((4, 128, 512), BF16),
             vmem((4, 256, 512), BF16),
-            dma((8,)), dma((8,)), dma((2,)), dma((3,)),
+            dma((8,)), dma((8,)), dma((2,)), dma((4,)),
             dma, dma, dma, dma, dma, dma, dma, dma((8,)), dma((8,)), dma((8,)), dma, dma, dma, dma,
             dma, dma, dma, dma((4,)), dma,
         ],
-        compiler_params=pltpu.CompilerParams(has_side_effects=True, collective_id=0),
+        compiler_params=pltpu.CompilerParams(has_side_effects=True, collective_id=0, vmem_limit_bytes=51 * 2**20),
         cost_estimate=pl.CostEstimate(
             flops=6 * 10**9, bytes_accessed=10 * 2**20, transcendentals=0
         ),

time: 73.7 us -> 70.9 us (0.962)
  Pallas kernels: 69.1 us -> 66.7 us
    pallas_call x1, Pallas kernels: 69.1 us -> 66.7 us  [shards(): pl.pallas_call(kernel, out_shape=(jax.ShapeDtypeStruct((32, 1024), F32),...]
    unnamed x2 -> x6, local copies, waits for them, and re-layouts: 3.83 us -> 3.34 us
where the time goes in v3:
time: 70.9 us; the launch traced here: 70.7 us
  Pallas kernels  66.7 us (94%)
  local copies, waits for them, and re-layouts  3.34 us (5%)
    pallas_call x1, Pallas kernels, shards(): pl.pallas_call(kernel, out_shape=(jax.ShapeDtypeStruct((32, 1024), F32),...  66.7 us
    unnamed x6, local copies, waits for them, and re-layouts  3.34 us

profile of v3, /device:TPU:1, one launch (start us, length us, event | category | flops | bytes accessed | tf_op | source)
XLA Modules:
  0.0 70.7 jit_solution(1936811173499391087)
XLA Ops:
  0.6 0.0 copy-start
  0.6 1.0 %copy-done = bf16[256,1024]{1,0:T(8,128)(2,1)S(1)} copy-done((bf16[256,1024]{1,0:T(8,128)(2,1)S(1)}, bf16[256,1024]{1,0:T(8,128)(2,1)}, u32[]{:S(2)}) %copy-start) | copy-done | bytes 524312
  1.7 0.0 copy-start.1
  1.7 0.7 copy-done.1
  2.4 66.7 %shard_map.77 = (f32[32,1024]{1,0:T(8,128)S(1)}, bf16[4,256,512]{2,1,0:T(8,128)(2,1)S(1)}) custom-call(bf16[256,4096]{1,0:T(8,128)(2,1)} %x_hbm.1, bf16[256,1024]{1,0:T(8,128)(2,1)S(1)} %copy-done, bf16[4,512,512]{2,1,0:T(8,128)(2,1)} %left_hbm.1, bf16[4,512,512]{2,1,0:T(8,128)(2,1)} %grads_hbm.1, bf16[4,512,512]{2,1,0:T(8,128)(2,1)} %right_hbm.1, ...), custom_call_target="tpu_custom_call" | custom-call | flops 6000000000 | bytes 10485760 | tf_op jit(solution)/shard_map/pallas_call | solution.py:358
  69.1 0.7 copy.10
  69.7 1.0 %copy.11 = bf16[4,256,512]{2,1,0:T(8,128)(2,1)} copy(bf16[4,256,512]{2,1,0:T(8,128)(2,1)S(1)} %get-tuple-element.5) | data formatting | bytes 2097152
Async XLA Ops:
  0.6 1.0 %copy-start = (bf16[256,1024]{1,0:T(8,128)(2,1)S(1)}, bf16[256,1024]{1,0:T(8,128)(2,1)}, u32[]{:S(2)}) copy-start(bf16[256,1024]{1,0:T(8,128)(2,1)} %kg_hbm.1) | copy-start | bytes 1572868
  1.7 0.7 copy-start.1

commit v4 on v3

--- a/solution.py
+++ b/solution.py
@@ -16,6 +16,7 @@
 NZ, NX, NY = 8, 4, 4
 NSH = 128
 LAGS = (2, 4, 6)
+AHEAD = 2
 COMPACT = 7
 
 
@@ -78,12 +79,20 @@
         pl.semaphore_signal(barrier, inc=1, device_id=there, device_id_type=MESH)
 
     def greet_all(k, carry):
-        @pl.when(k > 0)
-        def _():
-            greet(peer(k, 0))
-
-        for m in range(1, 16):
-            greet(peer(k, m))
+        dz = 4 + (k + 1) // 2 * (1 - 2 * lax.rem(k, 2))
+        tz = lax.rem(z + dz, NZ)
+        for dy in (2, 1, 3, 0):
+            for dl in (1, 0):
+                for dc in (1, 0):
+                    there = (e, tz, lax.rem(l + dl, 2), lax.rem(y + dy, 4), lax.rem(c + dc, 2))
+                    if dy or dl or dc:
+                        greet(there)
+                    else:
+
+                        @pl.when(k < NZ - 1)
+                        def _():
+                            greet(there)
+
         return carry
 
     for there in ((1 - e, z, l, y, c), (1 - e, z, l, y, 1 - c), (1 - e, z, 1 - l, y, c)):
@@ -133,10 +142,6 @@
         drain(left_v, w_sem.at[i])
     parts = []
     for j in range(2):
-        if j == 1:
-            pl.semaphore_wait(barrier, NSH + 2)
-            remote(key_half(1 - c), kgs.at[my_rows, :], send_key, kg_sem.at[1], partner)
-            lax.fori_loop(0, NZ, swap, 0)
         hit = mine_row & ((slot_row >> 2) == me) & ((k_row >> 1) == j)
         s = jnp.sum(jnp.where(hit, slot_row & 3, 0))
         half = dot(left_v[s], grads_v[s]).astype(BF16)
@@ -151,6 +156,10 @@
         stacked = jnp.concatenate([p[q * 128 : (q + 1) * 128] for p in parts], axis=0)
         moved = dot(perm, stacked).astype(BF16)
         prod[pl.ds(q * 32, 32)] = moved.reshape(32, 8, 512)
+
+    pl.semaphore_wait(barrier, NSH + 2)
+    remote(key_half(1 - c), kgs.at[my_rows, :], send_key, kg_sem.at[1], partner)
+    lax.fori_loop(0, NZ, swap, 0)
 
     def y_first(k, h):
         return (k >= 0) if h == 0 else (k < 0)
@@ -206,7 +215,7 @@
     drain(kgs.at[my_rows, :], kg_sem.at[0])
     drain(kgs.at[my_rows, :], kg_sem.at[1])
 
-    def multiply(k):
+    def multiply(k, carry):
         drain(xs.at[k, my_rows, :], x_sem.at[k])
         drain(xs.at[k, my_rows, :], x_rsem.at[k])
         acc = dot_t(xs[k], kgs[...])
@@ -220,6 +229,14 @@
                         xx = xe * 2 + xl
                         piece = acc[base : base + 32, cols].astype(BF16)
                         t1[k, h, pick2(along_y, yy, xx), pick2(along_y, xx, yy)] = piece
+
+        @pl.when(k < AHEAD)
+        def _():
+            send_direct(k)
+
+        return carry
+
+    def send_direct(k):
         for h in range(2):
             along_y = y_first(k, h)
             p = pos(along_y)
@@ -290,7 +307,7 @@
     def steps(i, carry):
         @pl.when(i < NZ)
         def _():
-            multiply(i)
+            send_direct(i)
 
         @pl.when(within(i, LAGS[0], NZ))
         def _():
@@ -314,7 +331,8 @@
 
         return carry
 
-    lax.fori_loop(0, max(NZ + LAGS[1], NZ - 1 + LAGS[2]), steps, 0)
+    lax.fori_loop(0, NZ, multiply, 0)
+    lax.fori_loop(AHEAD, max(NZ + LAGS[1], NZ - 1 + LAGS[2]), steps, 0)
 
     def assemble(r, carry):
         drain(comp_in.at[r], sem_c.at[r])

time: 70.9 us -> 68.3 us (0.963)
  Pallas kernels: 66.7 us -> 64.2 us
    pallas_call x1, Pallas kernels: 66.7 us -> 64.2 us  [shards(): pl.pallas_call(kernel, out_shape=(jax.ShapeDtypeStruct((32, 1024), F32),...]
where the time goes in v4:
time: 68.3 us; the launch traced here: 68.2 us
  Pallas kernels  64.2 us (94%)
  local copies, waits for them, and re-layouts  3.34 us (5%)
    pallas_call x1, Pallas kernels, shards(): pl.pallas_call(kernel, out_shape=(jax.ShapeDtypeStruct((32, 1024), F32),...  64.2 us
    unnamed x6, local copies, waits for them, and re-layouts  3.34 us

profile of v4, /device:TPU:1, one launch (start us, length us, event | category | flops | bytes accessed | tf_op | source)
XLA Modules:
  0.0 68.2 jit_solution(5393025719905284390)
XLA Ops:
  0.6 0.0 copy-start
  0.6 1.0 %copy-done = bf16[256,1024]{1,0:T(8,128)(2,1)S(1)} copy-done((bf16[256,1024]{1,0:T(8,128)(2,1)S(1)}, bf16[256,1024]{1,0:T(8,128)(2,1)}, u32[]{:S(2)}) %copy-start) | copy-done | bytes 524312
  1.7 0.0 copy-start.1
  1.7 0.7 copy-done.1
  2.4 64.2 %shard_map.77 = (f32[32,1024]{1,0:T(8,128)S(1)}, bf16[4,256,512]{2,1,0:T(8,128)(2,1)S(1)}) custom-call(bf16[256,4096]{1,0:T(8,128)(2,1)} %x_hbm.1, bf16[256,1024]{1,0:T(8,128)(2,1)S(1)} %copy-done, bf16[4,512,512]{2,1,0:T(8,128)(2,1)} %left_hbm.1, bf16[4,512,512]{2,1,0:T(8,128)(2,1)} %grads_hbm.1, bf16[4,512,512]{2,1,0:T(8,128)(2,1)} %right_hbm.1, ...), custom_call_target="tpu_custom_call" | custom-call | flops 6000000000 | bytes 10485760 | tf_op jit(solution)/shard_map/pallas_call | solution.py:376
  66.6 0.7 copy.10
  67.2 1.0 %copy.11 = bf16[4,256,512]{2,1,0:T(8,128)(2,1)} copy(bf16[4,256,512]{2,1,0:T(8,128)(2,1)S(1)} %get-tuple-element.5) | data formatting | bytes 2097152
Async XLA Ops:
  0.6 1.0 %copy-start = (bf16[256,1024]{1,0:T(8,128)(2,1)S(1)}, bf16[256,1024]{1,0:T(8,128)(2,1)}, u32[]{:S(2)}) copy-start(bf16[256,1024]{1,0:T(8,128)(2,1)} %kg_hbm.1) | copy-start | bytes 1572868
  1.7 0.7 copy-start.1

commit v5 on v4

--- a/solution.py
+++ b/solution.py
@@ -15,7 +15,7 @@
 BF16 = jnp.bfloat16
 NZ, NX, NY = 8, 4, 4
 NSH = 128
-LAGS = (2, 4, 6)
+LAGS = (2, 4, 8)
 AHEAD = 2
 COMPACT = 7
 
@@ -305,13 +305,13 @@
         return (i >= lag) & (i < lag + count)
 
     def steps(i, carry):
+        @pl.when(within(i, LAGS[0], NZ))
+        def _():
+            relay(i - LAGS[0])
+
         @pl.when(i < NZ)
         def _():
             send_direct(i)
-
-        @pl.when(within(i, LAGS[0], NZ))
-        def _():
-            relay(i - LAGS[0])
 
         @pl.when(within(i, LAGS[1], NZ))
         def _():
@@ -349,10 +349,10 @@
             total = total + r3[k, h].astype(F32)
         fin[h] = total
     here = gk_out.at[:, pl.ds(pl.multiple_of((c * 2 + e) * 256, 256), 256)]
-    pltpu.make_async_copy(fin.at[c], here, loc_f).start()
+    remote(fin.at[1 - c], here, send_f, sem_f, (1 - e, z, l, y, 1 - c))
     remote(fin.at[c], here, send_f, sem_f, (1 - e, z, l, y, c))
     remote(fin.at[1 - c], here, send_f, sem_f, (e, z, l, y, 1 - c))
-    remote(fin.at[1 - c], here, send_f, sem_f, (1 - e, z, l, y, 1 - c))
+    pltpu.make_async_copy(fin.at[c], here, loc_f).start()
 
     assemble(3, 0)
     drain(fin.at[0], loc_f)

time: 68.3 us -> 68 us (level)
  no operation moved by 1% of the time
where the time goes in v5:
time: 68 us; the launch traced here: 67.8 us
  Pallas kernels  63.9 us (94%)
  local copies, waits for them, and re-layouts  3.34 us (5%)
    pallas_call x1, Pallas kernels, shards(): pl.pallas_call(kernel, out_shape=(jax.ShapeDtypeStruct((32, 1024), F32),...  63.9 us
    unnamed x6, local copies, waits for them, and re-layouts  3.34 us

profile of v5, /device:TPU:1, one launch (start us, length us, event | category | flops | bytes accessed | tf_op | source)
XLA Modules:
  0.0 67.8 jit_solution(13757282477961345592)
XLA Ops:
  0.6 0.0 copy-start
  0.6 1.0 %copy-done = bf16[256,1024]{1,0:T(8,128)(2,1)S(1)} copy-done((bf16[256,1024]{1,0:T(8,128)(2,1)S(1)}, bf16[256,1024]{1,0:T(8,128)(2,1)}, u32[]{:S(2)}) %copy-start) | copy-done | bytes 524312
  1.7 0.0 copy-start.1
  1.7 0.7 copy-done.1
  2.4 63.9 %shard_map.77 = (f32[32,1024]{1,0:T(8,128)S(1)}, bf16[4,256,512]{2,1,0:T(8,128)(2,1)S(1)}) custom-call(bf16[256,4096]{1,0:T(8,128)(2,1)} %x_hbm.1, bf16[256,1024]{1,0:T(8,128)(2,1)S(1)} %copy-done, bf16[4,512,512]{2,1,0:T(8,128)(2,1)} %left_hbm.1, bf16[4,512,512]{2,1,0:T(8,128)(2,1)} %grads_hbm.1, bf16[4,512,512]{2,1,0:T(8,128)(2,1)} %right_hbm.1, ...), custom_call_target="tpu_custom_call" | custom-call | flops 6000000000 | bytes 10485760 | tf_op jit(solution)/shard_map/pallas_call | solution.py:376
  66.2 0.7 copy.10
  66.9 1.0 %copy.11 = bf16[4,256,512]{2,1,0:T(8,128)(2,1)} copy(bf16[4,256,512]{2,1,0:T(8,128)(2,1)S(1)} %get-tuple-element.5) | data formatting | bytes 2097152
Async XLA Ops:
  0.6 1.0 %copy-start = (bf16[256,1024]{1,0:T(8,128)(2,1)S(1)}, bf16[256,1024]{1,0:T(8,128)(2,1)}, u32[]{:S(2)}) copy-start(bf16[256,1024]{1,0:T(8,128)(2,1)} %kg_hbm.1) | copy-start | bytes 1572868
  1.7 0.7 %copy-start.1 = (s32[256]{0:T(256)S(1)}, s32[256]{0:T(256)}, u32[]{:S(2)}) copy-start(s32[256]{0:T(256)} %param.11) | copy-start | bytes 3076
